TPU v7x, 32 devices: a whole 2x2x4 slice. The times are simulated.
32 devices in a mesh: rows: 8 (over y, x, core), model: 4 (over z).
Axes of the slice: x: 2, y: 2, z: 4, core: 2. Of those that a mesh axis runs over, the one named last changes fastest.
Arguments:
- weight_gate: bfloat16 [2048, 8192], P('rows', 'model'), may hold values from -0.125 to 0.125
- low_gate: bfloat16 [2048, 64], P('rows'), may hold values from -0.125 to 0.125
- high_gate: bfloat16 [64, 8192], P(None, 'model'), may hold values from -0.75 to 0.75
- weight_up: bfloat16 [2048, 8192], P('rows', 'model'), may hold values from -0.125 to 0.125
- low_up: bfloat16 [2048, 64], P('rows'), may hold values from -0.125 to 0.125
- high_up: bfloat16 [64, 8192], P(None, 'model'), may hold values from -0.75 to 0.75
- weight_down: bfloat16 [8192, 2048], P('model', 'rows'), may hold values from -0.0625 to 0.0625
- low_down: bfloat16 [8192, 64], P('model'), may hold values from -0.0625 to 0.0625
- high_down: bfloat16 [64, 2048], P(None, 'rows'), may hold values from -0.75 to 0.75
- norm_train: float32 [2048], P(('rows', 'model')), may hold values from 0.25 to 1.75
- norm_step: float32 [2048], P(('rows', 'model')), may hold values from -0.3 to 0.3
Outputs:
- final_gate: bfloat16 [8192, 2048], P('model')
- final_up: bfloat16 [8192, 2048], P('model')
- final_down: bfloat16 [2048, 8192], P(None, 'model')
- serve_norm: bfloat16 [2048], replicated
All inputs are finite; a program needn't handle non-finite values.
Results may differ from a plain program's by a relative error of at most 0.001.
Values may be sent and summed in bfloat16 or wider, within the bound.
A program may use at most 192 MiB of HBM per device.

v0:
```python
import jax
import jax.numpy as jnp
from jax import lax
from jax.sharding import PartitionSpec as P

mix_rate = 0.5


def local(
    weight_gate,
    low_gate,
    high_gate,
    weight_up,
    low_up,
    high_up,
    weight_down,
    low_down,
    high_down,
    norm_train,
    norm_step,
):
    result_gate = weight_gate.astype(jnp.float32) + mix_rate * jnp.dot(
        low_gate, high_gate, preferred_element_type=jnp.float32
    )
    result_up = weight_up.astype(jnp.float32) + mix_rate * jnp.dot(
        low_up, high_up, preferred_element_type=jnp.float32
    )
    result_down = weight_down.astype(jnp.float32) + mix_rate * jnp.dot(
        low_down, high_down, preferred_element_type=jnp.float32
    )
    narrow_gate, narrow_up, narrow_down = (
        result_gate.astype(jnp.bfloat16),
        result_up.astype(jnp.bfloat16),
        result_down.astype(jnp.bfloat16),
    )
    final_gate, final_up, final_down = (
        lax.all_gather(narrow_gate, "rows", axis=0, tiled=True),
        lax.all_gather(narrow_up, "rows", axis=0, tiled=True),
        lax.all_gather(narrow_down, "rows", axis=1, tiled=True),
    )
    final_gate, final_up, final_down = (final_gate.T, final_up.T, final_down.T)
    serve_norm = lax.all_gather(
        (norm_train + norm_step).astype(jnp.bfloat16), ("rows", "model"), axis=0, tiled=True
    )
    return (final_gate, final_up, final_down, serve_norm)


def solution(mesh):
    in_specs = (
        P("rows", "model"),
        P("rows", None),
        P(None, "model"),
        P("rows", "model"),
        P("rows", None),
        P(None, "model"),
        P("model", "rows"),
        P("model", None),
        P(None, "rows"),
        P(("rows", "model")),
        P(("rows", "model")),
    )
    out_specs = (P("model", None), P("model", None), P(None, "model"), P())
    return jax.shard_map(local, mesh=mesh, in_specs=in_specs, out_specs=out_specs, check_vma=False)
```

profile of v0, /device:TPU:0, one launch (start us, length us, event | category | flops | bytes accessed | tf_op | source)
XLA Modules:
  0.0 202.2 jit_solution(15543596453073565614)
XLA Ops:
  7.2 0.0 copy-start
  7.2 0.0 copy-start.1
  7.2 0.0 copy-start.5
  7.2 0.0 copy-start.3
  7.2 0.0 all-gather.4.cloned.1.call-start
  7.3 0.9 copy-done
  8.1 2.7 %fusion.3 = bf16[256,2048]{1,0:T(8,128)(2,1)} fusion(bf16[256,64]{0,1:T(8,128)(2,1)} %param.12, bf16[64,2048]{1,0:T(8,128)(2,1)S(1)} %copy-done, bf16[256,2048]{1,0:T(8,128)(2,1)} %param.11), kind=kOutput, calls=%fused_computation.6 | convolution fusion | flops 69206016 | bytes 2392064 | tf_op jit(solution)/shard_map/dot_general | solution.py:22
  10.8 0.0 all-gather.4.cloned.1.call-update
  10.8 0.0 all-gather.6.cloned.1.call-start
  10.9 0.0 copy-done.1
  10.9 0.0 copy-done.5
  10.9 1.4 fusion.4
  12.3 0.0 all-gather.6.cloned.1.call-update
  12.4 0.0 all-gather.8.cloned.1.call-start
  12.4 1.5 fusion.5
  14.0 0.0 all-gather.8.cloned.1.call-update
  14.1 0.2 dynamic-update-slice
  14.3 42.9 %all-reduce = bf16[2048]{0:T(1024)(128)(2,1)} all-reduce(bf16[2048]{0:T(1024)(128)(2,1)S(1)} %dynamic-update-slice), channel_id=1, replica_groups=mesh['rows'=8,'model'=4] {'rows','model'}, use_global_device_ids=true, to_apply=%add | all-reduce | flops 2048 | bytes 8192
  57.3 11.7 %all-gather.4.cloned.1.call-done = bf16[2048,2048]{1,0:T(8,128)(2,1)} async-done(((bf16[256,2048]{1,0:T(8,128)(2,1)}), bf16[2048,2048]{1,0:T(8,128)(2,1)}) %all-gather.4.cloned.1.call-update) | async-done | bytes 8388624 | tf_op jit(solution)/shard_map/all_gather | solution.py:37
  69.0 12.3 %copy.15 = bf16[2048,2048]{1,0:T(8,128)(2,1)} copy(bf16[2048,2048]{0,1:T(8,128)(2,1)} %bitcast.9) | data formatting | bytes 16777216
  81.3 44.4 %all-gather.6.cloned.1.call-done = bf16[2048,2048]{1,0:T(8,128)(2,1)} async-done(((bf16[256,2048]{1,0:T(8,128)(2,1)}), bf16[2048,2048]{1,0:T(8,128)(2,1)}) %all-gather.6.cloned.1.call-update) | async-done | bytes 8388624 | tf_op jit(solution)/shard_map/all_gather | solution.py:38
  125.7 12.3 %copy.16 = bf16[2048,2048]{1,0:T(8,128)(2,1)} copy(bf16[2048,2048]{0,1:T(8,128)(2,1)} %bitcast.10) | data formatting | bytes 16777216
  137.9 45.5 %all-gather.8.cloned.1.call-done = bf16[2048,2048]{1,0:T(8,128)(2,1)} async-done(((bf16[2048,256]{1,0:T(8,128)(2,1)}), bf16[2048,2048]{1,0:T(8,128)(2,1)}) %all-gather.8.cloned.1.call-update) | async-done | bytes 8388624 | tf_op jit(solution)/shard_map/all_gather | solution.py:39
  183.4 12.2 %copy.17 = bf16[2048,2048]{1,0:T(8,128)(2,1)} copy(bf16[2048,2048]{0,1:T(8,128)(2,1)} %bitcast.11) | data formatting | bytes 16777216
  (13 shorter events, 0.0 us)
Async XLA Ops:
  7.2 1.0 copy-start
  7.2 3.7 %copy-start.1 = (bf16[256,2048]{1,0:T(8,128)(2,1)S(1)}, bf16[256,2048]{1,0:T(8,128)(2,1)}, u32[]{:S(2)}) copy-start(bf16[256,2048]{1,0:T(8,128)(2,1)} %param.14) | copy-start | bytes 3145732
  7.2 3.7 %copy-start.5 = (bf16[256,64]{0,1:T(8,128)(2,1)S(1)}, bf16[256,64]{0,1:T(8,128)(2,1)}, u32[]{:S(2)}) copy-start(bf16[256,64]{0,1:T(8,128)(2,1)} %param.15) | copy-start | bytes 98308
  7.2 3.7 %copy-start.3 = (bf16[64,2048]{1,0:T(8,128)(2,1)S(1)}, bf16[64,2048]{1,0:T(8,128)(2,1)}, u32[]{:S(2)}) copy-start(bf16[64,2048]{1,0:T(8,128)(2,1)} %param.16) | copy-start | bytes 786436
  7.2 61.8 %all-gather.4.cloned.1.call-start = ((), (), s32[]{:S(2)}) async-start(), calls=%async_computation | async-start | bytes 9437184 | tf_op jit(solution)/shard_map/all_gather | solution.py:37
  10.8 1.6 copy-start.2
  10.8 1.6 copy-start.4
  10.8 1.6 copy-start.6
  10.8 114.8 %all-gather.6.cloned.1.call-start = ((), (), s32[]{:S(2)}) async-start(), calls=%async_computation.1 | async-start | bytes 9437184 | tf_op jit(solution)/shard_map/all_gather | solution.py:38
  12.3 1.7 copy-start.7
  12.3 1.7 copy-start.8
  12.4 171.1 %all-gather.8.cloned.1.call-start = ((), (), s32[]{:S(2)}) async-start(), calls=%async_computation.2 | async-start | bytes 9437184 | tf_op jit(solution)/shard_map/all_gather | solution.py:39
Sparse Core Ops, SparseCore 0:
  10.9 58.0 all-gather.3
  71.5 54.1 all-gather.5
  127.5 55.8 all-gather.7
where the time goes:
time: 203 us; the launch traced here: 202 us
  waiting for transfers between devices  102 us (50%)
  blocking collectives  42.9 us (21%)
  local copies, waits for them, and re-layouts  37.9 us (19%)
  between operations  13.9 us (7%)
  matrix products  5.64 us (3%)
    all_gather x1, waiting for transfers between devices, local(): lax.all_gather(narrow_down, 'rows', axis=1, tiled=True)  45.5 us
    all_gather x1, waiting for transfers between devices, local(): lax.all_gather(narrow_up, 'rows', axis=0, tiled=True)  44.4 us
    unnamed x1, blocking collectives  42.9 us
    unnamed x23, local copies, waits for them, and re-layouts  37.9 us
    all_gather x1, waiting for transfers between devices, local(): lax.all_gather(narrow_gate, 'rows', axis=0, tiled=True)  11.7 us
  transfers between devices with their start and end apart: 3, of which 3 were waited for; matrix products, arithmetic and copies ran while one was open for 14% of the time, Pallas kernels for 0%

commit v1 on v0

v1 whole, which is shorter than its diff:
```python
import functools

import jax
import jax.numpy as jnp
from jax import lax
from jax.experimental import pallas as pl
from jax.experimental.pallas import tpu as pltpu
from jax.sharding import PartitionSpec as P

mix_rate = 0.5
MESH = pl.DeviceIdType.MESH
PIECES = 4
SIDE = 2


def gather_kernel(
    rows,
    model,
    *refs,
):
    sources, (og, ou, od, norm), refs = refs[:11], refs[11:15], refs[15:]
    held, refs = refs[:11], refs[11:]
    wg, lg, hg, wu, lu, hu, wd, ld, hd, nt, ns = held
    fetch_sem, link_send, link_recv, pair_send, pair_recv, norm_send, norm_recv = refs
    me = lax.axis_index("rows")
    depth = lax.axis_index("model")
    core = lax.rem(me, 2)
    x = lax.rem(me // 2, SIDE)
    y = me // (2 * SIDE)

    def device(y, x, core):
        return (y * SIDE + x) * 2 + core

    pair = device(y, x, 1 - core)
    near_x = device(y, 1 - x, core)
    near_y = device(1 - y, x, core)
    far = device(1 - y, 1 - x, core)

    def shifted(position, size, step):
        return lax.rem(position + step, size)

    barrier = pltpu.get_barrier_semaphore()
    for step in range(1, rows):
        pl.semaphore_signal(barrier, inc=1, device_id={"rows": shifted(me, rows, step)}, device_id_type=MESH)
    for step in range(1, model):
        pl.semaphore_signal(barrier, inc=1, device_id={"model": shifted(depth, model, step)}, device_id_type=MESH)

    outs = (og, ou, od)
    fetches = {}

    def fetch(key, i, *cut):
        fetches[key] = pltpu.make_async_copy(
            sources[i].at[cut] if cut else sources[i], held[i].at[cut] if cut else held[i],
            fetch_sem.at[len(fetches)],
        )

    long = wg.shape[1] // PIECES
    long_down = wd.shape[0] // PIECES
    short = wg.shape[0]
    short_down = wd.shape[1]
    units = [(a, k) for k in range(PIECES) for a in range(3)]

    for u, (a, k) in enumerate(units):
        if k == 0:
            fetch(("low", a), 3 * a + 1)
            fetch(("high", a), 3 * a + 2)
        if a < 2:
            fetch(u, 3 * a, pl.ds(0, short), pl.ds(k * long, long))
        else:
            fetch(u, 3 * a, pl.ds(k * long_down, long_down), pl.ds(0, short_down))
    fetch("train", 9)
    fetch("step", 10)
    for f in fetches.values():
        f.start()

    def place(u, owner):
        a, k = units[u]
        if a < 2:
            return outs[a].at[pl.ds(k * long, long), pl.ds(pl.multiple_of(owner * short, short), short)]
        return outs[a].at[pl.ds(pl.multiple_of(owner * short_down, short_down), short_down), pl.ds(k * long_down, long_down)]

    def compute(u):
        a, k = units[u]
        if k == 0:
            fetches["low", a].wait()
            fetches["high", a].wait()
        fetches[u].wait()
        if a < 2:
            w, low, high = ((wg, lg, hg), (wu, lu, hu))[a]
            cut = slice(k * long, (k + 1) * long)
            weight, low, high = w[:, cut], low[...], high[:, cut]
        else:
            cut = slice(k * long_down, (k + 1) * long_down)
            weight, low, high = wd[cut, :], ld[:, cut], hd[...]
        merged = weight.astype(jnp.float32) + mix_rate * lax.dot_general(
            low, high, (((0,), (0,)), ((), ())), preferred_element_type=jnp.float32
        )
        place(u, me)[...] = merged.astype(jnp.bfloat16).T

    def copy(u, owner, send, recv, target):
        return pltpu.make_async_remote_copy(
            src_ref=place(u, owner), dst_ref=place(u, owner), send_sem=send, recv_sem=recv,
            device_id={"rows": target}, device_id_type=MESH,
        )

    def link(lane, u, owner, target):
        return copy(u, owner, link_send.at[lane, u], link_recv.at[lane, u], target)

    def across(lane, u, owner):
        return copy(u, owner, pair_send.at[lane, u], pair_recv.at[lane, u], pair)

    def send_own(u):
        link(0, u, me, near_x).start()
        link(1, u, me, near_y).start()
        across(3, u, me).start()

    count = len(units)
    compute(0)
    fetches["train"].wait()
    fetches["step"].wait()
    norm[me, depth] = jnp.zeros(norm.shape[2:], norm.dtype)
    norm[me, depth, :, : nt.shape[1]] = nt[...] + ns[...]
    pl.semaphore_wait(barrier, rows - 1 + model - 1)
    for u in range(1, count):
        compute(u)
        send_own(u - 1)

    def norm_copy(step, send):
        if step < model:
            to = {"model": shifted(depth, model, step)}
            ref = norm.at[me, depth] if send else norm.at[me, shifted(depth, model, model - step)]
            slot = step - 1
        else:
            step = step - model + 1
            to = {"rows": shifted(me, rows, step)}
            ref = norm.at[me] if send else norm.at[shifted(me, rows, rows - step)]
            slot = model - 1 + step - 1
        return pltpu.make_async_remote_copy(
            src_ref=ref, dst_ref=ref, send_sem=norm_send.at[slot], recv_sem=norm_recv.at[slot],
            device_id=to, device_id_type=MESH,
        )

    for step in range(1, model):
        norm_copy(step, True).start()
    send_own(count - 1)
    for step in range(1, model):
        norm_copy(step, False).wait_recv()
    for step in range(model, model + rows - 1):
        norm_copy(step, True).start()

    for u in range(count):
        link(0, u, near_x, near_x).wait_recv()
        if u % 2 == 0:
            link(2, u, near_x, near_y).start()
        across(0, u, near_x).start()
        link(1, u, near_y, near_y).wait_recv()
        if u % 2 == 1:
            link(2, u, near_y, near_x).start()
        across(1, u, near_y).start()
    for u in range(count):
        link(2, u, far, near_x).wait_recv()
        across(2, u, far).start()

    for step in range(model, model + rows - 1):
        norm_copy(step, False).wait_recv()
    for step in range(1, model + rows - 1):
        norm_copy(step, True).wait_send()
    pair_x, pair_y = device(y, 1 - x, 1 - core), device(1 - y, x, 1 - core)
    pair_far = device(1 - y, 1 - x, 1 - core)
    for u in range(count):
        link(0, u, me, near_x).wait_send()
        link(1, u, me, near_y).wait_send()
        link(2, u, near_x if u % 2 == 0 else near_y, near_x).wait_send()
        for lane, mine, theirs in ((3, me, pair), (0, near_x, pair_x), (1, near_y, pair_y), (2, far, pair_far)):
            across(lane, u, mine).wait_send()
            across(lane, u, theirs).wait_recv()


def gathered(rows, model, arrays):
    weight_gate, weight_up, weight_down, norm_train = arrays[0], arrays[3], arrays[6], arrays[9]
    shapes = [
        (weight_gate.shape[1], weight_gate.shape[0] * rows),
        (weight_up.shape[1], weight_up.shape[0] * rows),
        (weight_down.shape[1] * rows, weight_down.shape[0]),
    ]
    lanes = -(-norm_train.shape[1] // 128) * 128
    count = 3 * PIECES
    small = rows - 1 + model - 1
    dma = pltpu.SemaphoreType.DMA
    vmem = pl.BlockSpec(memory_space=pltpu.VMEM)
    return pl.pallas_call(
        functools.partial(gather_kernel, rows, model),
        out_shape=[pltpu.VMEM(s, jnp.bfloat16) for s in shapes] + [pltpu.VMEM((rows, model, 1, lanes), jnp.float32)],
        in_specs=[pl.BlockSpec(memory_space=pltpu.HBM)] * len(arrays),
        out_specs=[vmem] * 4,
        scratch_shapes=[pltpu.VMEM(a.shape, a.dtype) for a in arrays]
        + [
            dma((count + 8,)),
            dma((3, count)), dma((3, count)), dma((4, count)), dma((4, count)), dma((small,)), dma((small,)),
        ],
        compiler_params=pltpu.CompilerParams(collective_id=0, has_side_effects=True, vmem_limit_bytes=39 * 2**20 + 5 * 2**17),
    )(*arrays)


def write_kernel(g, u, d, og, ou, od, sems):
    copies = [pltpu.make_async_copy(s, t, sems.at[i]) for i, (s, t) in enumerate(((g, og), (u, ou), (d, od)))]
    for c in copies:
        c.start()
    for c in copies:
        c.wait()


def written(arrays):
    return pl.pallas_call(
        write_kernel,
        out_shape=[jax.ShapeDtypeStruct(a.shape, a.dtype) for a in arrays],
        in_specs=[pl.BlockSpec(memory_space=pltpu.VMEM)] * 3,
        out_specs=[pl.BlockSpec(memory_space=pltpu.HBM)] * 3,
        scratch_shapes=[pltpu.SemaphoreType.DMA((3,))],
        compiler_params=pltpu.CompilerParams(vmem_limit_bytes=2**20),
    )(*arrays)


def local_kernel(rows, model, *arrays):
    arrays = tuple(a.T if i in (1, 4, 7) else a for i, a in enumerate(arrays[:9])) + tuple(
        a.reshape(1, -1) for a in arrays[9:]
    )
    gate, up, down, norm = gathered(rows, model, arrays)
    norm_size = arrays[9].shape[1]
    serve_norm = norm[:, :, 0, :norm_size].astype(jnp.bfloat16).reshape(-1)
    gate, up, down = written((gate, up, down))
    return gate, up, down, serve_norm


def merge(weight, low, high):
    full = weight.astype(jnp.float32) + mix_rate * jnp.dot(low, high, preferred_element_type=jnp.float32)
    return full.astype(jnp.bfloat16).T


def local_plain(*arrays):
    gate, up, down = merge(*arrays[:3]), merge(*arrays[3:6]), merge(*arrays[6:9])
    return (
        lax.all_gather(gate, "rows", axis=1, tiled=True),
        lax.all_gather(up, "rows", axis=1, tiled=True),
        lax.all_gather(down, "rows", axis=0, tiled=True),
        lax.all_gather((arrays[9] + arrays[10]).astype(jnp.bfloat16), ("rows", "model"), axis=0, tiled=True),
    )


def solution(mesh):
    rows, model = mesh.shape["rows"], mesh.shape["model"]
    local = functools.partial(local_kernel, rows, model) if rows == 2 * SIDE * SIDE else local_plain
    in_specs = (
        P("rows", "model"), P("rows", None), P(None, "model"),
        P("rows", "model"), P("rows", None), P(None, "model"),
        P("model", "rows"), P("model", None), P(None, "rows"),
        P(("rows", "model")), P(("rows", "model")),
    )
    out_specs = (P("model", None), P("model", None), P(None, "model"), P())
    return jax.shard_map(local, mesh=mesh, in_specs=in_specs, out_specs=out_specs, check_vma=False)
```

time: 203 us -> 122 us (0.60)
  Pallas kernels: 0 us -> 121 us
  waiting for transfers between devices: 102 us -> 0 us
  blocking collectives: 42.9 us -> 0 us
  local copies, waits for them, and re-layouts: 37.9 us -> 0.73 us
  between operations: 13.9 us -> 0.65 us
  matrix products: 5.64 us -> 0 us
    pallas_call x0 -> x2, Pallas kernels: none -> 121 us  [the longest x1 112 us: gathered(): pl.pallas_call(functools.partial(gather_kernel, rows, model), out_shape=[...]
    all_gather x3 -> x0, waiting for transfers between devices: 102 us -> none  [the longest x1 45.5 us: local(): lax.all_gather(narrow_down, 'rows', axis=1, tiled=True)]
    unnamed x1 -> x0, blocking collectives: 42.9 us -> none
    unnamed x23 -> x0, local copies, waits for them, and re-layouts: 37.9 us -> none
    dot_general x3 -> x0, matrix products: 5.64 us -> none  [the longest x1 2.67 us: local(): jnp.dot(low_gate, high_gate, preferred_element_type=jnp.float32)]
  transfers between devices with their start and end apart: 3 -> 0, of which waited for: 3 -> 0; matrix products, arithmetic and copies ran while one was open for 14% -> 0% of each run, Pallas kernels for 0% -> 0%
where the time goes in v1:
time: 122 us
  Pallas kernels  121 us (99%)
    pallas_call x1, Pallas kernels, gathered(): pl.pallas_call(functools.partial(gather_kernel, rows, model), out_shape=[...  112 us
    pallas_call x1, Pallas kernels, written(): pl.pallas_call(write_kernel, out_shape=[jax.ShapeDtypeStruct(a.shape, a.d...  8.71 us

profile of v1, /device:TPU:0, one launch (start us, length us, event | category | flops | bytes accessed | tf_op | source)
XLA Modules:
  0.0 122.2 jit_solution(1873034188070129180)
XLA Ops:
  0.6 112.1 %shard_map.138 = (bf16[2048,2048]{1,0:T(8,128)(2,1)S(1)}, bf16[2048,2048]{1,0:T(8,128)(2,1)S(1)}, bf16[2048,2048]{1,0:T(8,128)(2,1)S(1)}, f32[8,4,1,128]{3,2,1,0:T(1,128)S(1)}) custom-call(bf16[256,2048]{1,0:T(8,128)(2,1)} %refs_0_.1, bf16[64,256]{1,0:T(8,128)(2,1)} %bitcast.6, bf16[64,2048]{1,0:T(8,128)(2,1)} %refs_2_.1, bf16[256,2048]{1,0:T(8,128)(2,1)} %refs_3_.1, ...), custom_call_target="tpu_custom_call" | custom-call | tf_op jit(solution)/shard_map/pallas_call | solution.py:191
  112.8 8.7 %shard_map.139 = (bf16[2048,2048]{1,0:T(8,128)(2,1)}, bf16[2048,2048]{1,0:T(8,128)(2,1)}, bf16[2048,2048]{1,0:T(8,128)(2,1)}) custom-call(bf16[2048,2048]{1,0:T(8,128)(2,1)S(1)} %get-tuple-element.11.g, bf16[2048,2048]{1,0:T(8,128)(2,1)S(1)} %get-tuple-element.12.u, bf16[2048,2048]{1,0:T(8,128)(2,1)S(1)} %get-tuple-element.13.d), custom_call_target="tpu_custom_call" | custom-call | tf_op jit(solution)/shard_map/pallas_call | solution.py:214
  121.5 0.1 fusion
  121.6 0.7 convert_element_type.5

commit v2 on v1

--- a/solution.py
+++ b/solution.py
@@ -10,6 +10,7 @@
 mix_rate = 0.5
 MESH = pl.DeviceIdType.MESH
 PIECES = 4
+STRIPS = 1
 SIDE = 2
 
 
@@ -202,21 +203,35 @@
     )(*arrays)
 
 
-def write_kernel(g, u, d, og, ou, od, sems):
-    copies = [pltpu.make_async_copy(s, t, sems.at[i]) for i, (s, t) in enumerate(((g, og), (u, ou), (d, od)))]
+def write_kernel(size, lanes, g, u, d, norm, og, ou, od, out, sems):
+    strip = g.shape[0] // STRIPS
+    copies = [
+        pltpu.make_async_copy(s.at[pl.ds(k * strip, strip)], t.at[pl.ds(k * strip, strip)], sems.at[i, k])
+        for k in range(STRIPS)
+        for i, (s, t) in enumerate(((g, og), (u, ou), (d, od)))
+    ]
     for c in copies:
         c.start()
+    rows, model = norm.shape[:2]
+    parts = [norm[r, m][:, :size] for r in range(rows) for m in range(model)]
+    group = lanes // size
+    packed = [jnp.concatenate(parts[i : i + group], axis=1) for i in range(0, len(parts), group)]
+    out[...] = jnp.concatenate(packed, axis=0).astype(out.dtype)
     for c in copies:
         c.wait()
 
 
-def written(arrays):
+def written(size, arrays):
+    lanes = arrays[3].shape[3]
+    total = arrays[3].shape[0] * arrays[3].shape[1] * size
+    hbm, vmem = pl.BlockSpec(memory_space=pltpu.HBM), pl.BlockSpec(memory_space=pltpu.VMEM)
     return pl.pallas_call(
-        write_kernel,
-        out_shape=[jax.ShapeDtypeStruct(a.shape, a.dtype) for a in arrays],
-        in_specs=[pl.BlockSpec(memory_space=pltpu.VMEM)] * 3,
-        out_specs=[pl.BlockSpec(memory_space=pltpu.HBM)] * 3,
-        scratch_shapes=[pltpu.SemaphoreType.DMA((3,))],
+        functools.partial(write_kernel, size, lanes),
+        out_shape=[jax.ShapeDtypeStruct(a.shape, a.dtype) for a in arrays[:3]]
+        + [jax.ShapeDtypeStruct((total // lanes, lanes), jnp.bfloat16)],
+        in_specs=[vmem] * 4,
+        out_specs=[hbm] * 3 + [vmem],
+        scratch_shapes=[pltpu.SemaphoreType.DMA((3, STRIPS))],
         compiler_params=pltpu.CompilerParams(vmem_limit_bytes=2**20),
     )(*arrays)
 
@@ -226,10 +241,8 @@
         a.reshape(1, -1) for a in arrays[9:]
     )
     gate, up, down, norm = gathered(rows, model, arrays)
-    norm_size = arrays[9].shape[1]
-    serve_norm = norm[:, :, 0, :norm_size].astype(jnp.bfloat16).reshape(-1)
-    gate, up, down = written((gate, up, down))
-    return gate, up, down, serve_norm
+    gate, up, down, serve_norm = written(arrays[9].shape[1], (gate, up, down, norm))
+    return gate, up, down, serve_norm.reshape(-1)
 
 
 def merge(weight, low, high):

time: 122 us -> 122 us (level)
  no operation moved by 1% of the time
where the time goes in v2:
time: 122 us
  Pallas kernels  121 us (99%)
    pallas_call x1, Pallas kernels, gathered(): pl.pallas_call(functools.partial(gather_kernel, rows, model), out_shape=[...  112 us
    pallas_call x1, Pallas kernels, written(): pl.pallas_call(functools.partial(write_kernel, size, lanes), out_shape=[j...  9.3 us

profile of v2, /device:TPU:0, one launch (start us, length us, event | category | flops | bytes accessed | tf_op | source)
XLA Modules:
  0.0 122.1 jit_solution(7022164548023786989)
XLA Ops:
  0.6 112.1 %shard_map.138 = (bf16[2048,2048]{1,0:T(8,128)(2,1)S(1)}, bf16[2048,2048]{1,0:T(8,128)(2,1)S(1)}, bf16[2048,2048]{1,0:T(8,128)(2,1)S(1)}, f32[8,4,1,128]{3,2,1,0:T(1,128)S(1)}) custom-call(bf16[256,2048]{1,0:T(8,128)(2,1)} %refs_0_.1, bf16[64,256]{1,0:T(8,128)(2,1)} %bitcast.7, bf16[64,2048]{1,0:T(8,128)(2,1)} %refs_2_.1, bf16[256,2048]{1,0:T(8,128)(2,1)} %refs_3_.1, ...), custom_call_target="tpu_custom_call" | custom-call | tf_op jit(solution)/shard_map/pallas_call | solution.py:192
  112.8 9.3 %shard_map.139 = (bf16[2048,2048]{1,0:T(8,128)(2,1)}, bf16[2048,2048]{1,0:T(8,128)(2,1)}, bf16[2048,2048]{1,0:T(8,128)(2,1)}, bf16[16,128]{1,0:T(8,128)(2,1)}) custom-call(bf16[2048,2048]{1,0:T(8,128)(2,1)S(1)} %get-tuple-element.12.g, bf16[2048,2048]{1,0:T(8,128)(2,1)S(1)} %get-tuple-element.13.u, bf16[2048,2048]{1,0:T(8,128)(2,1)S(1)} %get-tuple-element.14.d, ...), custom_call_target="tpu_custom_call" | custom-call | tf_op jit(solution)/shard_map/pallas_call | solution.py:228
